TPU v7x, 32 devices: a whole 2x2x4 slice. The times are simulated.
32 devices in a mesh: wide: 8 (over z, core), narrow: 4 (over y, x).
Axes of the slice: x: 2, y: 2, z: 4, core: 2. Of those that a mesh axis runs over, the one named last changes fastest.
Arguments:
- activations: bfloat16 [512, 16384], P(None, 'wide'), may hold values from -6 to 6
- enc_weight: bfloat16 [16384, 4096], P('wide', 'narrow'), may hold values from -0.046875 to 0.046875
- enc_bias: float32 [4096], P('narrow'), may hold values from -4 to 4
- dec_weight: bfloat16 [4096, 16384], P('narrow', 'wide'), may hold values from -0.375 to 0.375
- dec_bias: float32 [16384], P('wide'), may hold values from -4 to 4
- active_ids: int32 [512, 64], replicated, may hold values from 0 to 4095, all different within a row
Outputs:
- dec_grad: bfloat16 [4096, 16384], P('narrow', 'wide')
- latent_grad: float32 [512, 4096], P('wide', 'narrow')
Inputs may be any that keep to these rules, and one draw needn't show every extreme that they name: `active_ids`: each row names 64 different latents; every latent is named by some row.
All inputs are finite; a program needn't handle non-finite values.
Results may differ from a plain program's by a relative error of at most 0.0058.
Values may be sent and summed in bfloat16 or wider, within the bound.
A program may use at most 128 MiB of HBM per device.

v0:
```python
import jax
import jax.numpy as jnp
from jax import lax
from jax.sharding import PartitionSpec as P


def prefix(value, axis, combine, identity):
    length, position = (lax.axis_size(axis), lax.axis_index(axis))
    everything = jax.tree.map(
        lambda part, kind: lax.all_gather(part.astype(kind), axis),
        value,
        (jnp.bfloat16, jnp.bfloat16),
    )
    start = jax.tree.map(
        lambda part, zero: jnp.broadcast_to(jnp.asarray(zero, part.dtype), part.shape),
        value,
        identity,
    )

    def hop(k, before):
        reached = k < position
        new = combine(
            before, jax.tree.map(lambda part, own: part[k].astype(own.dtype), everything, value)
        )
        return jax.tree.map(lambda a, b: jnp.where(reached, a, b), new, before)

    return lax.fori_loop(0, length, hop, start)


def add_fields(earlier, later):
    return jax.tree.map(jnp.add, earlier, later)


def local(activations, enc_weight, enc_bias, dec_weight, dec_bias, active_ids):
    token_count = activations.shape[0]
    latent_width = enc_weight.shape[1]
    groups = lax.axis_size("narrow")
    group_index = lax.axis_index("narrow")
    first_latent = group_index * latent_width
    inside = (active_ids >= first_latent) & (active_ids < first_latent + latent_width)
    local_ids = jnp.where(inside, active_ids - first_latent, latent_width)
    row_index = jnp.arange(token_count, dtype=jnp.int32)[:, None]
    active_mask = (
        jnp.zeros((token_count, latent_width), jnp.float32)
        .at[row_index, local_ids]
        .set(1.0, mode="drop")
    )
    share_rows = token_count // lax.axis_size("wide")
    offset = lax.axis_index("wide") * share_rows
    own_mask = lax.dynamic_slice_in_dim(active_mask, offset, share_rows, 0)
    partial_pre = jnp.dot(activations, enc_weight, preferred_element_type=jnp.float32)
    preact = lax.psum(partial_pre, "wide") + enc_bias
    latents = (active_mask * preact).astype(jnp.bfloat16)
    recon_part = jnp.dot(latents, dec_weight, preferred_element_type=jnp.float32)
    target = activations.astype(jnp.float32)
    nothing = jnp.zeros_like(recon_part)
    position = group_index.astype(jnp.float32)
    lower_sum, lower_weighted = prefix(
        (recon_part, position * recon_part), "narrow", add_fields, (nothing, nothing)
    )
    weighted_sum = lax.psum((groups - position) * recon_part, "narrow")
    suffix = (
        (groups - position) * dec_bias
        + weighted_sum
        - position * lower_sum
        + lower_weighted
        - (groups - position) * target
    )
    errors = (suffix / groups).astype(jnp.bfloat16)
    dec_grad = lax.dot_general(
        latents, errors, (((0,), (0,)), ((), ())), preferred_element_type=jnp.float32
    ).astype(jnp.bfloat16)
    latent_rows = lax.psum_scatter(
        lax.dot_general(
            errors, dec_weight, (((1,), (1,)), ((), ())), preferred_element_type=jnp.float32
        ),
        "wide",
        scatter_dimension=0,
        tiled=True,
    )
    latent_out = own_mask * latent_rows
    return (dec_grad, latent_out)


def solution(mesh):
    in_specs = (
        P(None, "wide"),
        P("wide", "narrow"),
        P("narrow"),
        P("narrow", "wide"),
        P("wide"),
        P(),
    )
    out_specs = (P("narrow", "wide"), P("wide", "narrow"))
    return jax.shard_map(local, mesh=mesh, in_specs=in_specs, out_specs=out_specs, check_vma=False)
```

profile of v0, /device:TPU:0, one launch (start us, length us, event | category | flops | bytes accessed | tf_op | source)
XLA Modules:
  0.0 489.2 jit_solution(10238089520648462262)
XLA Ops:
  7.2 0.0 all-reduce.3.cloned.1.call-start
  7.2 6.5 %fusion.3 = f32[512,1024]{1,0:T(8,128)} fusion(bf16[512,2048]{1,0:T(8,128)(2,1)} %param.8, bf16[2048,1024]{1,0:T(8,128)(2,1)} %param.9), kind=kOutput, calls=%fused_computation.18 | convolution fusion | flops 2147483648 | bytes 8388608 | tf_op jit(solution)/shard_map/dot_general | solution.py:51
  13.8 0.0 all-gather.5.cloned.1.call-start
  13.9 0.1 multiply_reduce_fusion
  14.0 0.1 and_reduce_fusion
  14.2 0.1 copy.8
  14.3 0.1 reshape.18
  14.4 121.4 %scatter_custom_fusion = f32[524288]{0:T(1024)} fusion(s32[32768]{0:T(1024)S(1)} %reshape.18, f32[32768]{0:T(1024)S(1)} %broadcast.15, f32[]{:T(128)} %constant.43.clone.1), kind=kCustom, calls=%fused_computation.8 | custom fusion | bytes 2097156
  135.9 1.7 reshape.15
  137.6 0.0 all-reduce.3.cloned.1.call-done
  137.7 2.2 multiply_convert_fusion.2
  139.9 0.6 copy-done.6
  140.5 5.6 %broadcast_multiply_fusion = (f32[512,2048]{1,0:T(8,128)}, bf16[512,2048]{1,0:T(8,128)(2,1)}, bf16[512,2048]{1,0:T(8,128)(2,1)}) fusion(f32[]{:T(128)S(6)} %sub.16, f32[]{:T(128)S(6)} %convert_element_type.42, bf16[512,1024]{1,0:T(8,128)(2,1)S(1)} %multiply_convert_fusion.2, bf16[1024,2048]{1,0:T(8,128)(2,1)S(1)} %copy-done.6), kind=kOutput, calls=%fused_computation.6 | convolution fusion | flops 2151677952 | bytes 13631496 | tf_op jit(solution)/shard_map/dot_general | solution.py:54
  146.1 0.0 all-gather.7.cloned.1.call-start
  146.2 0.7 all-gather.7.cloned.1.call-update
  146.9 0.0 all-reduce.5.cloned.1.call-start
  146.9 0.5 all-reduce.5.cloned.1.call-update
  147.4 0.2 reduce-scatter.2.cloned.1.call-start
  147.7 88.8 %all-gather.5.cloned.1.call-done = bf16[2048,2048]{1,0:T(8,128)(2,1)} async-done(((bf16[512,2048]{1,0:T(8,128)(2,1)}), bf16[2048,2048]{1,0:T(8,128)(2,1)}) %all-gather.5.cloned.1.call-update) | async-done | bytes 8388624 | tf_op jit(solution)/shard_map/all_gather | solution.py:10
  236.5 89.4 %all-gather.7.cloned.1.call-done = bf16[2048,2048]{1,0:T(8,128)(2,1)} async-done(((bf16[512,2048]{1,0:T(8,128)(2,1)}), bf16[2048,2048]{1,0:T(8,128)(2,1)}) %all-gather.7.cloned.1.call-update) | async-done | bytes 8388624 | tf_op jit(solution)/shard_map/all_gather | solution.py:10
  325.8 39.3 %while.16 = (s32[]{:T(128)}, f32[512,2048]{1,0:T(8,128)}, f32[512,2048]{1,0:T(8,128)}, s32[]{:T(128)}, bf16[4,512,2048]{2,1,0:T(8,128)(2,1)}, /*index=5*/bf16[4,512,2048]{2,1,0:T(8,128)(2,1)}, s32[]{:T(128)}, s32[]{:T(128)}) while((s32[]{:T(128)}, f32[512,2048]{1,0:T(8,128)}, f32[512,2048]{1,0:T(8,128)}, s32[]{:T(128)}, ...), condition=%wide.region_4.5_spmd.clone, body=%wide.region_3.4_spmd.clone.sunk | while | flops 8388612 | bytes 20971628 | solution.py:27
  325.8 7.8 %add_select_fusion.3 = (f32[512,2048]{1,0:T(8,128)}, f32[512,2048]{1,0:T(8,128)}) fusion(f32[512,2048]{1,0:T(8,128)} %get-tuple-element.204, bf16[4,512,2048]{2,1,0:T(8,128)(2,1)} %get-tuple-element.215, s32[]{:T(128)} %get-tuple-element.202, pred[]{:T(512)S(6)} %compare.7, pred[]{:T(512)S(6)} %lt.50, bf16[4,512,2048]{2,1,0:T(8,128)(2,1)} %get-tuple-element.214, ...), kind=kLoop, calls=%fused_computation.1.clone.1 | loop fusion | flops 8388608 | bytes 20971526 | tf_op jit(solution)/shard_map/while/body/eval_jaxpr/jit(_where)/select_n | solution.py:25
  333.6 10.8 %add_select_fusion.3 = (f32[512,2048]{1,0:T(8,128)}, f32[512,2048]{1,0:T(8,128)}) fusion(f32[512,2048]{1,0:T(8,128)} %get-tuple-element.204, bf16[4,512,2048]{2,1,0:T(8,128)(2,1)} %get-tuple-element.215, s32[]{:T(128)} %get-tuple-element.202, pred[]{:T(512)S(6)} %compare.7, pred[]{:T(512)S(6)} %lt.50, bf16[4,512,2048]{2,1,0:T(8,128)(2,1)} %get-tuple-element.214, ...), kind=kLoop, calls=%fused_computation.1.clone.1 | loop fusion | flops 8388608 | bytes 20971526 | tf_op jit(solution)/shard_map/while/body/eval_jaxpr/jit(_where)/select_n | solution.py:25
  344.4 10.4 %add_select_fusion.3 = (f32[512,2048]{1,0:T(8,128)}, f32[512,2048]{1,0:T(8,128)}) fusion(f32[512,2048]{1,0:T(8,128)} %get-tuple-element.204, bf16[4,512,2048]{2,1,0:T(8,128)(2,1)} %get-tuple-element.215, s32[]{:T(128)} %get-tuple-element.202, pred[]{:T(512)S(6)} %compare.7, pred[]{:T(512)S(6)} %lt.50, bf16[4,512,2048]{2,1,0:T(8,128)(2,1)} %get-tuple-element.214, ...), kind=kLoop, calls=%fused_computation.1.clone.1 | loop fusion | flops 8388608 | bytes 20971526 | tf_op jit(solution)/shard_map/while/body/eval_jaxpr/jit(_where)/select_n | solution.py:25
  354.8 10.3 %add_select_fusion.3 = (f32[512,2048]{1,0:T(8,128)}, f32[512,2048]{1,0:T(8,128)}) fusion(f32[512,2048]{1,0:T(8,128)} %get-tuple-element.204, bf16[4,512,2048]{2,1,0:T(8,128)(2,1)} %get-tuple-element.215, s32[]{:T(128)} %get-tuple-element.202, pred[]{:T(512)S(6)} %compare.7, pred[]{:T(512)S(6)} %lt.50, bf16[4,512,2048]{2,1,0:T(8,128)(2,1)} %get-tuple-element.214, ...), kind=kLoop, calls=%fused_computation.1.clone.1 | loop fusion | flops 8388608 | bytes 20971526 | tf_op jit(solution)/shard_map/while/body/eval_jaxpr/jit(_where)/select_n | solution.py:25
  365.1 67.5 %all-reduce.5.cloned.1.call-done = f32[512,2048]{1,0:T(8,128)} async-done(((f32[512,2048]{1,0:T(8,128)}), f32[512,2048]{1,0:T(8,128)}) %all-reduce.5.cloned.1.call-update) | async-done | bytes 4194320 | tf_op jit(solution)/shard_map/psum | solution.py:61
  432.6 7.2 %multiply_convert_fusion = bf16[512,2048]{1,0:T(8,128)(2,1)S(1)} fusion(bf16[512,2048]{1,0:T(8,128)(2,1)} %param.8, f32[512,2048]{1,0:T(8,128)} %get-tuple-element.113, f32[512,2048]{1,0:T(8,128)} %get-tuple-element.112, f32[512,2048]{1,0:T(8,128)} %all-reduce.5.cloned.1.call-done, f32[]{:T(128)S(6)} %convert_element_type.42, f32[]{:T(128)S(6)} %sub.16, ...), kind=kLoop, calls=%fused_computation.3 | loop fusion | flops 9437184 | bytes 16785416 | tf_op jit(solution)/shard_map/convert_element_type | solution.py:69
  439.8 1.3 copy-done
  441.1 3.7 fusion.4
  444.8 6.0 %convolution_convert_fusion = bf16[1024,2048]{1,0:T(8,128)(2,1)} fusion(bf16[512,1024]{1,0:T(8,128)(2,1)S(1)} %multiply_convert_fusion.2, bf16[512,2048]{1,0:T(8,128)(2,1)} %copy-done), kind=kOutput, calls=%fused_computation.5 | convolution fusion | flops 2149580800 | bytes 7340032 | tf_op jit(solution)/shard_map/dot_general | solution.py:70
  450.8 30.2 %reduce-scatter.2.cloned.1.call-done = f32[64,1024]{1,0:T(8,128)} async-done(((f32[512,1024]{1,0:T(8,128)}), f32[64,1024]{1,0:T(8,128)}) %reduce-scatter.2.cloned.1.call-update) | async-done | bytes 262160 | tf_op jit(solution)/shard_map/reduce_scatter | solution.py:73
  481.0 1.7 dynamic-slice_multiply_fusion
  (24 shorter events, 0.2 us)
Async XLA Ops:
  7.2 6.8 %copy-start.5 = (s32[2]{0:T(128)S(1)}, s32[2]{0:T(128)}, u32[]{:S(2)}) copy-start(s32[2]{0:T(128)} %constant.54) | copy-start | bytes 28
  7.2 6.8 %copy-start.4 = (s32[2]{0:T(128)S(1)}, s32[2]{0:T(128)}, u32[]{:S(2)}) copy-start(s32[2]{0:T(128)} %constant.57) | copy-start | bytes 28
  7.2 6.6 %copy-start.1 = (s32[512,64]{0,1:T(8,128)S(1)}, s32[512,64]{0,1:T(8,128)}, u32[]{:S(2)}) copy-start(s32[512,64]{0,1:T(8,128)} %param.13) | copy-start | bytes 393220
  7.2 130.4 %all-reduce.3.cloned.1.call-start = ((), (), s32[]{:S(2)}) async-start(), calls=%async_computation.1 | async-start | bytes 4194304 | tf_op jit(solution)/shard_map/psum | solution.py:52
  13.8 222.7 %all-gather.5.cloned.1.call-start = ((), (), s32[]{:S(2)}) async-start(), calls=%async_computation.4 | async-start | bytes 10485760 | tf_op jit(solution)/shard_map/all_gather | solution.py:10
  13.9 123.8 %copy-start.3 = (f32[1024]{0:T(1024)S(1)}, f32[1024]{0:T(1024)}, u32[]{:S(2)}) copy-start(f32[1024]{0:T(1024)} %param.10) | copy-start | bytes 12292
  137.6 2.8 copy-start.6
  146.1 1.6 copy-start.2
  146.1 179.7 %all-gather.7.cloned.1.call-start = ((), (), s32[]{:S(2)}) async-start(), calls=%async_computation.5 | async-start | bytes 10485760 | tf_op jit(solution)/shard_map/all_gather | solution.py:10
  146.9 285.8 %all-reduce.5.cloned.1.call-start = ((), (), s32[]{:S(2)}) async-start(), calls=%async_computation.2 | async-start | bytes 8388608 | tf_op jit(solution)/shard_map/psum | solution.py:61
  147.4 333.6 %reduce-scatter.2.cloned.1.call-start = ((), (), s32[]{:S(2)}) async-start(), calls=%async_computation.3 | async-start | bytes 2359296 | tf_op jit(solution)/shard_map/reduce_scatter | solution.py:73
  432.6 8.5 %copy-start.7 = (bf16[1024,2048]{1,0:T(8,128)(2,1)S(1)}, bf16[1024,2048]{1,0:T(8,128)(2,1)}, u32[]{:S(2)}) copy-start(bf16[1024,2048]{1,0:T(8,128)(2,1)} %param.11) | copy-start | bytes 12582916
  439.8 1.3 copy-start
Sparse Core Ops, SparseCore 0:
  13.9 67.9 all-reduce.2
  146.2 90.1 all-gather.4
  238.3 87.4 all-gather.6
  329.0 103.5 all-reduce.4
  445.0 35.9 reduce-scatter.1
where the time goes:
time: 489 us
  waiting for transfers between devices  277 us (57%)
  local copies, waits for them, and re-layouts  125 us (26%)
  other arithmetic  50.6 us (10%)
  matrix products  21.8 us (4%)
  between operations  14 us (3%)
    all_gather x2, waiting for transfers between devices, prefix(): lax.all_gather(part.astype(kind), axis)  178 us
    unnamed x20, local copies, waits for them, and re-layouts  124 us
    psum x1, waiting for transfers between devices, local(): weighted_sum = lax.psum((groups - position) * recon_part, 'narrow')  67.5 us
    select_n x4, other arithmetic, hop(): return jax.tree.map(lambda a, b: jnp.where(reached, a, b), new, before)  39.3 us
    reduce_scatter x1, waiting for transfers between devices, local(): lax.psum_scatter(lax.dot_general(errors, dec_weight, (((1,), (1,)), ((),...  30.2 us
  transfers between devices with their start and end apart: 5, of which 4 were waited for; matrix products, arithmetic and copies ran while one was open for 35% of the time, Pallas kernels for 0%

commit v1 on v0

--- a/solution.py
+++ b/solution.py
@@ -58,7 +58,7 @@
     lower_sum, lower_weighted = prefix(
         (recon_part, position * recon_part), "narrow", add_fields, (nothing, nothing)
     )
-    weighted_sum = lax.psum((groups - position) * recon_part, "narrow")
+    weighted_sum = jnp.sum(lax.all_gather((groups - position) * recon_part, "narrow"), axis=0)
     suffix = (
         (groups - position) * dec_bias
         + weighted_sum

time: 489 us -> 552 us (1.13)
  waiting for transfers between devices: 277 us -> 328 us
  other arithmetic: 50.6 us -> 62.3 us
    all_gather x0 -> x1, waiting for transfers between devices: none -> 118 us  [local(): lax.all_gather((groups - position) * recon_part, 'narrow')]
    psum x1 -> x0, waiting for transfers between devices: 67.5 us -> none  [local(): weighted_sum = lax.psum((groups - position) * recon_part, 'narrow')]
    reduce_sum x0 -> x1, other arithmetic: none -> 10.1 us  [local(): jnp.sum(lax.all_gather((groups - position) * recon_part, 'narrow'), axis=0)]
  transfers between devices with their start and end apart: 5 -> 5, of which waited for: 4 -> 4; matrix products, arithmetic and copies ran while one was open for 35% -> 31% of each run, Pallas kernels for 0% -> 0%
where the time goes in v1:
time: 552 us
  waiting for transfers between devices  328 us (59%)
  local copies, waits for them, and re-layouts  125 us (23%)
  other arithmetic  62.3 us (11%)
  matrix products  21.9 us (4%)
  between operations  14 us (3%)
    all_gather x2, waiting for transfers between devices, prefix(): lax.all_gather(part.astype(kind), axis)  178 us
    unnamed x20, local copies, waits for them, and re-layouts  124 us
    all_gather x1, waiting for transfers between devices, local(): lax.all_gather((groups - position) * recon_part, 'narrow')  118 us
    select_n x4, other arithmetic, hop(): return jax.tree.map(lambda a, b: jnp.where(reached, a, b), new, before)  40.8 us
    reduce_scatter x1, waiting for transfers between devices, local(): lax.psum_scatter(lax.dot_general(errors, dec_weight, (((1,), (1,)), ((),...  30.2 us
  transfers between devices with their start and end apart: 5, of which 4 were waited for; matrix products, arithmetic and copies ran while one was open for 31% of the time, Pallas kernels for 0%

profile of v1, /device:TPU:0, one launch (start us, length us, event | category | flops | bytes accessed | tf_op | source)
XLA Modules:
  0.0 551.7 jit_solution(18410821786554459092)
XLA Ops:
  7.2 0.0 all-reduce.2.cloned.1.call-start
  7.2 6.5 %fusion.3 = f32[512,1024]{1,0:T(8,128)} fusion(bf16[512,2048]{1,0:T(8,128)(2,1)} %param.8, bf16[2048,1024]{1,0:T(8,128)(2,1)} %param.9), kind=kOutput, calls=%fused_computation.18 | convolution fusion | flops 2147483648 | bytes 8388608 | tf_op jit(solution)/shard_map/dot_general | solution.py:51
  13.8 0.0 all-gather.9.cloned.1.call-start
  13.9 0.1 multiply_reduce_fusion
  14.0 0.1 and_reduce_fusion
  14.2 0.1 copy.8
  14.3 0.1 reshape.18
  14.4 121.4 %scatter_custom_fusion = f32[524288]{0:T(1024)} fusion(s32[32768]{0:T(1024)S(1)} %reshape.18, f32[32768]{0:T(1024)S(1)} %broadcast.15, f32[]{:T(128)} %constant.44.clone.1), kind=kCustom, calls=%fused_computation.8 | custom fusion | bytes 2097156
  135.9 1.7 reshape.15
  137.7 2.2 multiply_convert_fusion.2
  139.9 0.6 copy-done.6
  140.5 5.7 %broadcast_multiply_fusion = (f32[512,2048]{1,0:T(8,128)}, bf16[512,2048]{1,0:T(8,128)(2,1)}, bf16[512,2048]{1,0:T(8,128)(2,1)}) fusion(f32[]{:T(128)S(6)} %sub.16, f32[]{:T(128)S(6)} %convert_element_type.42, bf16[512,1024]{1,0:T(8,128)(2,1)S(1)} %multiply_convert_fusion.2, bf16[1024,2048]{1,0:T(8,128)(2,1)S(1)} %copy-done.6), kind=kOutput, calls=%fused_computation.6 | convolution fusion | flops 2151677952 | bytes 13631496 | tf_op jit(solution)/shard_map/dot_general | solution.py:54
  146.2 0.0 all-gather.11.cloned.1.call-start
  146.2 0.7 all-gather.11.cloned.1.call-update
  146.9 0.0 all-gather.7.cloned.1.call-start
  147.0 0.5 all-gather.7.cloned.1.call-update
  147.5 0.2 reduce-scatter.2.cloned.1.call-start
  147.8 88.8 %all-gather.9.cloned.1.call-done = bf16[2048,2048]{1,0:T(8,128)(2,1)} async-done(((bf16[512,2048]{1,0:T(8,128)(2,1)}), bf16[2048,2048]{1,0:T(8,128)(2,1)}) %all-gather.9.cloned.1.call-update) | async-done | bytes 8388624 | tf_op jit(solution)/shard_map/all_gather | solution.py:10
  236.5 89.4 %all-gather.11.cloned.1.call-done = bf16[2048,2048]{1,0:T(8,128)(2,1)} async-done(((bf16[512,2048]{1,0:T(8,128)(2,1)}), bf16[2048,2048]{1,0:T(8,128)(2,1)}) %all-gather.11.cloned.1.call-update) | async-done | bytes 8388624 | tf_op jit(solution)/shard_map/all_gather | solution.py:10
  325.9 40.8 %while.16 = (s32[]{:T(128)}, f32[512,2048]{1,0:T(8,128)}, f32[512,2048]{1,0:T(8,128)}, s32[]{:T(128)}, bf16[4,512,2048]{2,1,0:T(8,128)(2,1)}, /*index=5*/bf16[4,512,2048]{2,1,0:T(8,128)(2,1)}, s32[]{:T(128)}, s32[]{:T(128)}) while((s32[]{:T(128)}, f32[512,2048]{1,0:T(8,128)}, f32[512,2048]{1,0:T(8,128)}, s32[]{:T(128)}, ...), condition=%wide.region_4.5_spmd.clone, body=%wide.region_3.4_spmd.clone.sunk | while | flops 8388612 | bytes 20971628 | solution.py:27
  325.9 7.8 %add_select_fusion.3 = (f32[512,2048]{1,0:T(8,128)}, f32[512,2048]{1,0:T(8,128)}) fusion(f32[512,2048]{1,0:T(8,128)} %get-tuple-element.204, bf16[4,512,2048]{2,1,0:T(8,128)(2,1)} %get-tuple-element.215, s32[]{:T(128)} %get-tuple-element.202, pred[]{:T(512)S(6)} %compare.7, pred[]{:T(512)S(6)} %lt.50, bf16[4,512,2048]{2,1,0:T(8,128)(2,1)} %get-tuple-element.214, ...), kind=kLoop, calls=%fused_computation.1.clone.1 | loop fusion | flops 8388608 | bytes 20971526 | tf_op jit(solution)/shard_map/while/body/eval_jaxpr/jit(_where)/select_n | solution.py:25
  333.7 12.7 %add_select_fusion.3 = (f32[512,2048]{1,0:T(8,128)}, f32[512,2048]{1,0:T(8,128)}) fusion(f32[512,2048]{1,0:T(8,128)} %get-tuple-element.204, bf16[4,512,2048]{2,1,0:T(8,128)(2,1)} %get-tuple-element.215, s32[]{:T(128)} %get-tuple-element.202, pred[]{:T(512)S(6)} %compare.7, pred[]{:T(512)S(6)} %lt.50, bf16[4,512,2048]{2,1,0:T(8,128)(2,1)} %get-tuple-element.214, ...), kind=kLoop, calls=%fused_computation.1.clone.1 | loop fusion | flops 8388608 | bytes 20971526 | tf_op jit(solution)/shard_map/while/body/eval_jaxpr/jit(_where)/select_n | solution.py:25
  346.3 10.2 %add_select_fusion.3 = (f32[512,2048]{1,0:T(8,128)}, f32[512,2048]{1,0:T(8,128)}) fusion(f32[512,2048]{1,0:T(8,128)} %get-tuple-element.204, bf16[4,512,2048]{2,1,0:T(8,128)(2,1)} %get-tuple-element.215, s32[]{:T(128)} %get-tuple-element.202, pred[]{:T(512)S(6)} %compare.7, pred[]{:T(512)S(6)} %lt.50, bf16[4,512,2048]{2,1,0:T(8,128)(2,1)} %get-tuple-element.214, ...), kind=kLoop, calls=%fused_computation.1.clone.1 | loop fusion | flops 8388608 | bytes 20971526 | tf_op jit(solution)/shard_map/while/body/eval_jaxpr/jit(_where)/select_n | solution.py:25
  356.5 10.2 %add_select_fusion.3 = (f32[512,2048]{1,0:T(8,128)}, f32[512,2048]{1,0:T(8,128)}) fusion(f32[512,2048]{1,0:T(8,128)} %get-tuple-element.204, bf16[4,512,2048]{2,1,0:T(8,128)(2,1)} %get-tuple-element.215, s32[]{:T(128)} %get-tuple-element.202, pred[]{:T(512)S(6)} %compare.7, pred[]{:T(512)S(6)} %lt.50, bf16[4,512,2048]{2,1,0:T(8,128)(2,1)} %get-tuple-element.214, ...), kind=kLoop, calls=%fused_computation.1.clone.1 | loop fusion | flops 8388608 | bytes 20971526 | tf_op jit(solution)/shard_map/while/body/eval_jaxpr/jit(_where)/select_n | solution.py:25
  366.7 118.2 %all-gather.7.cloned.1.call-done = f32[2048,2048]{1,0:T(8,128)} async-done(((f32[512,2048]{1,0:T(8,128)}), f32[2048,2048]{1,0:T(8,128)}) %all-gather.7.cloned.1.call-update) | async-done | bytes 16777232 | tf_op jit(solution)/shard_map/all_gather | solution.py:61
  484.9 10.1 %reduce_sum.9 = f32[512,2048]{1,0:T(8,128)} reduce(f32[4,512,2048]{2,1,0:T(8,128)} %bitcast.21, f32[]{:T(128)} %constant.44.clone.1), dimensions={0}, to_apply=%region_2.3 | reduce | flops 3145728 | bytes 20971524 | tf_op jit(solution)/shard_map/reduce_sum | solution.py:61
  495.0 7.2 %multiply_convert_fusion = bf16[512,2048]{1,0:T(8,128)(2,1)S(1)} fusion(bf16[512,2048]{1,0:T(8,128)(2,1)} %param.8, f32[512,2048]{1,0:T(8,128)} %get-tuple-element.113, f32[512,2048]{1,0:T(8,128)} %get-tuple-element.112, f32[512,2048]{1,0:T(8,128)} %reduce_sum.9, f32[]{:T(128)S(6)} %convert_element_type.42, f32[]{:T(128)S(6)} %sub.16, ...), kind=kLoop, calls=%fused_computation.3 | loop fusion | flops 9437184 | bytes 16785416 | tf_op jit(solution)/shard_map/convert_element_type | solution.py:69
  502.2 1.3 copy-done
  503.5 3.7 fusion.4
  507.3 6.0 %convolution_convert_fusion = bf16[1024,2048]{1,0:T(8,128)(2,1)} fusion(bf16[512,1024]{1,0:T(8,128)(2,1)S(1)} %multiply_convert_fusion.2, bf16[512,2048]{1,0:T(8,128)(2,1)} %copy-done), kind=kOutput, calls=%fused_computation.5 | convolution fusion | flops 2149580800 | bytes 7340032 | tf_op jit(solution)/shard_map/dot_general | solution.py:70
  513.3 30.2 %reduce-scatter.2.cloned.1.call-done = f32[64,1024]{1,0:T(8,128)} async-done(((f32[512,1024]{1,0:T(8,128)}), f32[64,1024]{1,0:T(8,128)}) %reduce-scatter.2.cloned.1.call-update) | async-done | bytes 262160 | tf_op jit(solution)/shard_map/reduce_scatter | solution.py:73
  543.5 1.7 dynamic-slice_multiply_fusion
  (25 shorter events, 0.2 us)
Async XLA Ops:
  7.2 6.8 %copy-start.5 = (s32[2]{0:T(128)S(1)}, s32[2]{0:T(128)}, u32[]{:S(2)}) copy-start(s32[2]{0:T(128)} %constant.55) | copy-start | bytes 28
  7.2 6.8 %copy-start.4 = (s32[2]{0:T(128)S(1)}, s32[2]{0:T(128)}, u32[]{:S(2)}) copy-start(s32[2]{0:T(128)} %constant.58) | copy-start | bytes 28
  7.2 6.6 %copy-start.1 = (s32[512,64]{0,1:T(8,128)S(1)}, s32[512,64]{0,1:T(8,128)}, u32[]{:S(2)}) copy-start(s32[512,64]{0,1:T(8,128)} %param.13) | copy-start | bytes 393220
  7.2 130.4 %all-reduce.2.cloned.1.call-start = ((), (), s32[]{:S(2)}) async-start(), calls=%async_computation.1 | async-start | bytes 4194304 | tf_op jit(solution)/shard_map/psum | solution.py:52
  13.8 222.8 %all-gather.9.cloned.1.call-start = ((), (), s32[]{:S(2)}) async-start(), calls=%async_computation.4 | async-start | bytes 10485760 | tf_op jit(solution)/shard_map/all_gather | solution.py:10
  13.9 123.8 %copy-start.3 = (f32[1024]{0:T(1024)S(1)}, f32[1024]{0:T(1024)}, u32[]{:S(2)}) copy-start(f32[1024]{0:T(1024)} %param.10) | copy-start | bytes 12292
  137.6 2.8 copy-start.6
  146.2 1.6 copy-start.2
  146.2 179.7 %all-gather.11.cloned.1.call-start = ((), (), s32[]{:S(2)}) async-start(), calls=%async_computation.5 | async-start | bytes 10485760 | tf_op jit(solution)/shard_map/all_gather | solution.py:10
  146.9 338.0 %all-gather.7.cloned.1.call-start = ((), (), s32[]{:S(2)}) async-start(), calls=%async_computation.3 | async-start | bytes 20971520 | tf_op jit(solution)/shard_map/all_gather | solution.py:61
  147.5 396.0 %reduce-scatter.2.cloned.1.call-start = ((), (), s32[]{:S(2)}) async-start(), calls=%async_computation.2 | async-start | bytes 2359296 | tf_op jit(solution)/shard_map/reduce_scatter | solution.py:73
  495.0 8.5 %copy-start.7 = (bf16[1024,2048]{1,0:T(8,128)(2,1)S(1)}, bf16[1024,2048]{1,0:T(8,128)(2,1)}, u32[]{:S(2)}) copy-start(bf16[1024,2048]{1,0:T(8,128)(2,1)} %param.11) | copy-start | bytes 12582916
  502.2 1.3 copy-start
Sparse Core Ops, SparseCore 0:
  13.9 67.9 all-reduce.1
  146.3 90.1 all-gather.8
  238.4 87.4 all-gather.10
  327.6 157.2 all-gather.6
  507.4 36.0 reduce-scatter.1
